TPU v7x, 32 devices: a whole 2x2x4 slice. The times are simulated.
32 devices in a mesh: dp: 4 (over y, x), row: 4 (over z), col: 2 (over core).
Axes of the slice: x: 2, y: 2, z: 4, core: 2. Of those that a mesh axis runs over, the one named last changes fastest.
Arguments:
- activations: bfloat16 [4, 64, 128, 512], P('dp', None, 'row', 'col'), may hold values from -18 to 18
- kernel: bfloat16 [3, 3, 64, 64], replicated, may hold values from -0.125 to 0.125
- gain: float32 [64], replicated, may hold values from 0.25 to 1.75
- cotangent: bfloat16 [4, 64, 128, 512], P('dp', None, 'row', 'col'), may hold values from -16 to 16
Outputs:
- input_grad: bfloat16 [4, 64, 128, 512], P('dp', None, 'row', 'col')
- weight_grad: float32 [3, 3, 64, 64], P(None, None, 'dp')
- gain_grad: float32 [64], replicated
- shift_grad: float32 [64], replicated
All inputs are finite; a program needn't handle non-finite values.
Results may differ from a plain program's by a relative error of at most 0.0049.
Values may be sent and summed in bfloat16 or wider, within the bound.
A program may use at most 64 MiB of HBM per device.

v0:
```python
import jax
import jax.numpy as jnp
from jax import lax
from jax.sharding import PartitionSpec as P


def with_halo(shard, sides, width):
    for axis, dim in sides:
        count, length = (lax.axis_size(axis), shard.shape[dim])
        up = [(i, (i + 1) % count) for i in range(count - 1)]
        down = [(j, i) for i, j in up]
        last = lax.slice_in_dim(shard, length - width, length, axis=dim)
        initial = lax.slice_in_dim(shard, 0, width, axis=dim)
        before = lax.ppermute(last, axis, up)
        after = lax.ppermute(initial, axis, down)
        shard = jnp.concatenate([before, shard, after], axis=dim)
    return shard


def per_device(activations, kernel, gain, cotangent):
    images, channels, height, width = activations.shape
    total = jnp.float32(
        images * height * width * lax.axis_size("dp") * lax.axis_size("row") * lax.axis_size("col")
    )
    padded = with_halo(activations, (("row", 2), ("col", 3)), 1)
    pre = jnp.zeros((images, channels, height, width), jnp.float32)
    for tap_row in range(3):
        for tap_col in range(3):
            window = padded[:, :, tap_row : tap_row + height, tap_col : tap_col + width]
            pre = pre + jnp.einsum(
                "oc,bchw->bohw",
                kernel[tap_row, tap_col],
                window,
                preferred_element_type=jnp.float32,
            )
    grad = cotangent.astype(jnp.float32)
    local_pre = jnp.sum(pre, axis=(0, 2, 3))
    local_sq = jnp.sum(pre * pre, axis=(0, 2, 3))
    local_cot = jnp.sum(grad, axis=(0, 2, 3))
    local_cross = jnp.sum(grad * pre, axis=(0, 2, 3))
    sum_pre, sum_sq, sum_cot, sum_cross = lax.psum(
        (local_pre, local_sq, local_cot, local_cross), ("dp", "row", "col")
    )
    mean = sum_pre / total
    rstd = lax.rsqrt(sum_sq / total - mean * mean + 1e-05)
    sum_norm = (sum_cross - mean * sum_cot) * rstd
    normed = (pre - mean[:, None, None]) * rstd[:, None, None]
    pre_grad = (gain * rstd)[:, None, None] * (
        grad - (sum_cot / total)[:, None, None] - normed * (sum_norm / total)[:, None, None]
    )
    pre_grad = pre_grad.astype(jnp.bfloat16)
    grad_padded = with_halo(pre_grad, (("row", 2), ("col", 3)), 1)
    input_grad = jnp.zeros((images, channels, height, width), jnp.float32)
    kernel_terms = []
    for tap_row in range(3):
        for tap_col in range(3):
            shifted = grad_padded[
                :, :, 2 - tap_row : 2 - tap_row + height, 2 - tap_col : 2 - tap_col + width
            ]
            input_grad = input_grad + jnp.einsum(
                "oc,bohw->bchw",
                kernel[tap_row, tap_col],
                shifted,
                preferred_element_type=jnp.float32,
            )
            window = padded[:, :, tap_row : tap_row + height, tap_col : tap_col + width]
            kernel_terms.append(
                jnp.einsum("bohw,bchw->oc", pre_grad, window, preferred_element_type=jnp.float32)
            )
    factor = total ** (-0.5)
    local_kernel = jnp.stack(kernel_terms).reshape(3, 3, channels, channels) * factor
    spatial = lax.psum(local_kernel, ("row", "col"))
    weight_grad = lax.psum_scatter(spatial, "dp", scatter_dimension=2, tiled=True)
    return (input_grad.astype(jnp.bfloat16), weight_grad, sum_norm / total, sum_cot / total)


def solution(mesh):
    return jax.shard_map(
        per_device,
        mesh=mesh,
        in_specs=(P("dp", None, "row", "col"), P(), P(), P("dp", None, "row", "col")),
        out_specs=(P("dp", None, "row", "col"), P(None, None, "dp", None), P(), P()),
        check_vma=False,
    )
```

profile of v0, /device:TPU:0, one launch (start us, length us, event | category | flops | bytes accessed | tf_op | source)
XLA Modules:
  0.0 162.4 jit_solution(4085869104326707929)
XLA Ops:
  7.2 1.9 %copy.26 = bf16[1,64,32,256]{3,1,2,0:T(8,128)(2,1)S(1)} copy(bf16[1,64,32,256]{3,2,1,0:T(8,128)(2,1)} %param.4) | data formatting | bytes 2097152 | tf_op args[0]
  9.2 5.0 %collective-permute-start = (bf16[1,64,1,256]{3,1,2,0:T(8,128)(2,1)S(1)}, bf16[1,64,1,256]{3,1,2,0:T(8,128)(2,1)S(1)}, u32[]{:S(2)}, u32[]{:S(2)}) collective-permute-start(bf16[1,64,1,256]{3,1,2,0:T(8,128)(2,1)S(1)} %get-tuple-element.29), channel_id=1, source_target_pairs={{0,2},{2,4},{4,6},{1,3},{3,5},{5,7},{8,10},{10,12},{12,14},{9,11},... | collective-permute-start | bytes 98312 | tf_op jit(solution)/shard_map/ppermute | solution.py:14
  14.1 1.3 collective-permute-start.1
  15.4 2.2 %fusion.55 = f32[32,256,64]{1,2,0:T(8,128)} fusion(bf16[64,32,256]{2,1,0:T(8,128)(2,1)S(1)} %bitcast.222, bf16[3,3,64,64]{3,2,1,0:T(8,128)(2,1)S(1)} %copy-done.18), kind=kOutput, calls=%fused_computation.92 | convolution fusion | flops 67108864 | bytes 3162112 | tf_op jit(solution)/shard_map/oc,bchw->bohw/dot_general | solution.py:30
  18.3 1.7 %collective-permute-done.1 = bf16[1,64,1,256]{3,1,2,0:T(8,128)(2,1)S(1)} collective-permute-done((bf16[1,64,1,256]{3,1,2,0:T(8,128)(2,1)S(1)}, bf16[1,64,1,256]{3,1,2,0:T(8,128)(2,1)S(1)}, u32[]{:S(2)}, u32[]{:S(2)}) %collective-permute-start.1) | collective-permute-done | bytes 32800 | tf_op jit(solution)/shard_map/ppermute | solution.py:15
  22.2 3.0 %collective-permute-start.2 = (bf16[1,64,34,1]{1,2,3,0:T(8,128)(2,1)S(1)}, bf16[1,64,34,1]{1,2,3,0:T(8,128)(2,1)S(1)}, u32[]{:S(2)}, u32[]{:S(2)}) collective-permute-start(bf16[1,64,34,1]{1,2,3,0:T(8,128)(2,1)S(1)} %copy.29), channel_id=1, source_target_pairs={{0,1},{2,3},{4,5},{6,7},{8,9},{10,11},{12,13},{14,15},{16,17},{18,... | collective-permute-start | bytes 13064 | tf_op jit(solution)/shard_map/ppermute | solution.py:14
  25.2 1.8 %fusion.58 = f32[32,256,64]{1,2,0:T(8,128)} fusion(bf16[1,64,32,256]{3,1,2,0:T(8,128)(2,1)S(1)} %copy.26, bf16[1,64,1,256]{3,1,2,0:T(8,128)(2,1)S(1)} %collective-permute-done, bf16[3,3,64,64]{3,2,1,0:T(8,128)(2,1)S(1)} %copy-done.18), kind=kOutput, calls=%fused_computation.94 | convolution fusion | flops 69206016 | bytes 3194880 | tf_op jit(solution)/shard_map/oc,bchw->bohw/dot_general | solution.py:30
  27.0 1.7 %fusion.61 = f32[32,256,64]{1,2,0:T(8,128)} fusion(bf16[1,64,1,256]{3,1,2,0:T(8,128)(2,1)S(1)} %collective-permute-done.1, bf16[1,64,32,256]{3,1,2,0:T(8,128)(2,1)S(1)} %copy.26, bf16[3,3,64,64]{3,2,1,0:T(8,128)(2,1)S(1)} %copy-done.18), kind=kOutput, calls=%fused_computation.95 | convolution fusion | flops 69206016 | bytes 3194880 | tf_op jit(solution)/shard_map/oc,bchw->bohw/dot_general | solution.py:30
  29.1 2.1 %fusion.78 = f32[32,256,64]{1,2,0:T(8,128)} fusion(bf16[3,3,64,64]{3,2,1,0:T(8,128)(2,1)S(1)} %copy-done.18, bf16[1,64,34,256]{3,1,2,0:T(8,128)(2,1)S(1)} %constant_dynamic-update-slice_fusion, bf16[1,64,34,1]{3,1,2,0:T(8,128)(2,1)S(1)} %copy.33), kind=kOutput, calls=%fused_computation.109 | convolution fusion | flops 69206016 | bytes 3784704 | tf_op jit(solution)/shard_map/oc,bchw->bohw/dot_general | solution.py:30
  31.1 2.1 %fusion.86 = f32[32,256,64]{1,2,0:T(8,128)} fusion(bf16[3,3,64,64]{3,2,1,0:T(8,128)(2,1)S(1)} %copy-done.18, bf16[1,64,34,256]{3,1,2,0:T(8,128)(2,1)S(1)} %constant_dynamic-update-slice_fusion, bf16[1,64,34,1]{3,1,2,0:T(8,128)(2,1)S(1)} %copy.33), kind=kOutput, calls=%fused_computation.117 | convolution fusion | flops 69206016 | bytes 3784704 | tf_op jit(solution)/shard_map/oc,bchw->bohw/dot_general | solution.py:30
  38.3 3.8 %fusion.3 = (f32[64]{0:T(128)S(1)}, f32[64]{0:T(128)S(1)}, f32[64]{0:T(128)S(1)}, f32[32,256,64]{1,2,0:T(8,128)S(1)}) fusion(bf16[1,64,32,256]{3,2,1,0:T(8,128)(2,1)} %param.7, bf16[1,64,34,1]{3,1,2,0:T(8,128)(2,1)S(1)} %copy-done.2, bf16[1,64,34,256]{3,1,2,0:T(8,128)(2,1)S(1)} %constant_dynamic-update-slice_fusion, ...), kind=kOutput, calls=%fused_computation.6 | convolution fusion | flops 76545856 | bytes 21611264 | tf_op jit(solution)/shard_map/oc,bchw->bohw/dot_general | solution.py:30
  42.3 40.6 %all-reduce = (f32[64]{0:T(128)S(1)}, f32[64]{0:T(128)S(1)}, f32[64]{0:T(128)S(1)}, f32[64]{0:T(128)S(1)}) all-reduce(f32[64]{0:T(128)S(1)} %get-tuple-element.13, f32[64]{0:T(128)S(1)} %reduce_sum.37, f32[64]{0:T(128)S(1)} %get-tuple-element.12, f32[64]{0:T(128)S(1)} %get-tuple-element.14), channel_id=1, replica_groups=mesh['dp'=4,'row'=4,'col'=2] {'dp','row','col'}, use_global_device_ids=true, to_apply=%region_1.0 | all-reduce | flops 256 | bytes 2048 | tf_op jit(solution)/shard_map/psum | solution.py:41
  83.0 2.8 %fusion.2 = bf16[1,64,32,256]{3,1,2,0:T(8,128)(2,1)S(1)} fusion(f32[32,256,64]{1,2,0:T(8,128)} %copy-done, f32[64]{0:T(128)S(1)} %get-tuple-element.32, f32[64]{0:T(128)S(1)} %get-tuple-element.20, f32[64]{0:T(128)S(1)} %get-tuple-element.33, f32[64]{0:T(128)S(1)} %get-tuple-element.31, f32[64]{0:T(128)S(1)} %get-tuple-element.19, ...), kind=kLoop, calls=%fused_computation.5 | loop fusion | flops 4194304 | bytes 4195584 | tf_op jit(solution)/shard_map/convert_element_type | solution.py:51
  86.4 1.8 %fusion.52 = f32[32,256,64]{1,2,0:T(8,128)} fusion(bf16[1,64,32,256]{3,1,2,0:T(8,128)(2,1)S(1)} %fusion.2, bf16[3,3,64,64]{3,2,1,0:T(8,128)(2,1)S(1)} %copy-done.18), kind=kOutput, calls=%fused_computation.89 | convolution fusion | flops 67108864 | bytes 3162112 | tf_op jit(solution)/shard_map/oc,bohw->bchw/dot_general | solution.py:60
  91.2 1.3 fusion.11
  96.3 4.5 %collective-permute-start.4 = (bf16[1,64,1,256]{3,1,2,0:T(8,128)(2,1)S(1)}, bf16[1,64,1,256]{3,1,2,0:T(8,128)(2,1)S(1)}, u32[]{:S(2)}, u32[]{:S(2)}) collective-permute-start(bf16[1,64,1,256]{3,1,2,0:T(8,128)(2,1)S(1)} %get-tuple-element.28), channel_id=1, source_target_pairs={{0,2},{2,4},{4,6},{1,3},{3,5},{5,7},{8,10},{10,12},{12,14},{9,11},... | collective-permute-start | bytes 98312 | tf_op jit(solution)/shard_map/ppermute | solution.py:14
  104.8 3.2 %collective-permute-start.7 = (bf16[1,64,34,1]{1,2,3,0:T(8,128)(2,1)S(1)}, bf16[1,64,34,1]{1,2,3,0:T(8,128)(2,1)S(1)}, u32[]{:S(2)}, u32[]{:S(2)}) collective-permute-start(bf16[1,64,34,1]{1,2,3,0:T(8,128)(2,1)S(1)} %copy.41), channel_id=1, source_target_pairs={{0,1},{2,3},{4,5},{6,7},{8,9},{10,11},{12,13},{14,15},{16,17},{18,... | collective-permute-start | bytes 13064 | tf_op jit(solution)/shard_map/ppermute | solution.py:14
  108.1 1.8 %fusion.35 = f32[32,256,64]{1,2,0:T(8,128)} fusion(bf16[1,64,1,256]{3,1,2,0:T(8,128)(2,1)S(1)} %collective-permute-done.5, bf16[1,64,32,256]{3,1,2,0:T(8,128)(2,1)S(1)} %fusion.2, bf16[3,3,64,64]{3,2,1,0:T(8,128)(2,1)S(1)} %copy-done.18), kind=kOutput, calls=%fused_computation.68 | convolution fusion | flops 67633152 | bytes 3194880 | tf_op jit(solution)/shard_map/oc,bohw->bchw/dot_general | solution.py:60
  109.9 1.8 %fusion.27 = f32[32,256,64]{1,2,0:T(8,128)} fusion(bf16[1,64,32,256]{3,1,2,0:T(8,128)(2,1)S(1)} %fusion.2, bf16[1,64,1,256]{3,1,2,0:T(8,128)(2,1)S(1)} %collective-permute-done.4, bf16[3,3,64,64]{3,2,1,0:T(8,128)(2,1)S(1)} %copy-done.18), kind=kOutput, calls=%fused_computation.56 | convolution fusion | flops 67633152 | bytes 3194880 | tf_op jit(solution)/shard_map/oc,bohw->bchw/dot_general | solution.py:60
  112.5 1.4 maximum_maximum_fusion
  118.5 1.6 fusion.24
  120.1 1.6 copy.51
  121.6 3.8 %reduce-scatter.2.cloned.1.call-done = f32[3,3,16,64]{3,2,1,0:T(8,128)} async-done(((f32[3,3,64,64]{3,2,1,0:T(8,128)}), f32[3,3,16,64]{3,2,1,0:T(8,128)}) %reduce-scatter.2.cloned.1.call-update) | async-done | bytes 36880 | tf_op jit(solution)/shard_map/reduce_scatter | solution.py:73
  125.5 30.0 %psum.40 = f32[3,3,16,64]{3,2,1,0:T(8,128)} all-reduce(f32[3,3,16,64]{3,2,1,0:T(8,128)} %reduce-scatter.2.cloned.1.call-done), channel_id=1, replica_groups=mesh['dp'=4,'row'=4,'col'=2] {'row','col'}, use_global_device_ids=true, to_apply=%region_8.0 | all-reduce | flops 9216 | bytes 73728 | tf_op jit(solution)/shard_map/psum | solution.py:72
  (92 shorter events, 24.9 us)
Async XLA Ops:
  7.2 8.3 %copy-start.8 = (bf16[1,64,32,256]{3,2,1,0:T(8,128)(2,1)S(1)}, bf16[1,64,32,256]{3,2,1,0:T(8,128)(2,1)}, u32[]{:S(2)}) copy-start(bf16[1,64,32,256]{3,2,1,0:T(8,128)(2,1)} %param.4) | copy-start | bytes 3145732
  7.2 8.3 %copy-start.18 = (bf16[3,3,64,64]{3,2,1,0:T(8,128)(2,1)S(1)}, bf16[3,3,64,64]{3,2,1,0:T(8,128)(2,1)}, u32[]{:S(2)}) copy-start(bf16[3,3,64,64]{3,2,1,0:T(8,128)(2,1)} %param.5) | copy-start | bytes 221188
  7.2 118.3 %reduce-scatter.2.cloned.1.call-start = ((), (), s32[]{:S(2)}) async-start(), calls=%async_computation.1 | async-start | bytes 368640 | tf_op jit(solution)/shard_map/reduce_scatter | solution.py:73
  9.1 17.8 %copy-start.6 = (bf16[1,64,32,256]{3,1,2,0:T(8,128)(2,1)}, bf16[1,64,32,256]{3,1,2,0:T(8,128)(2,1)S(1)}, u32[]{:S(2)}) copy-start(bf16[1,64,32,256]{3,1,2,0:T(8,128)(2,1)S(1)} %copy.26) | copy-start | bytes 3145732
  9.2 8.5 %collective-permute-start = (bf16[1,64,1,256]{3,1,2,0:T(8,128)(2,1)S(1)}, bf16[1,64,1,256]{3,1,2,0:T(8,128)(2,1)S(1)}, u32[]{:S(2)}, u32[]{:S(2)}) collective-permute-start(bf16[1,64,1,256]{3,1,2,0:T(8,128)(2,1)S(1)} %get-tuple-element.29), channel_id=1, source_target_pairs={{0,2},{2,4},{4,6},{1,3},{3,5},{5,7},{8,10},{10,12},{12,14},{9,11},... | collective-permute-start | bytes 98312 | tf_op jit(solution)/shard_map/ppermute | solution.py:14
  14.1 5.8 %collective-permute-start.1 = (bf16[1,64,1,256]{3,1,2,0:T(8,128)(2,1)S(1)}, bf16[1,64,1,256]{3,1,2,0:T(8,128)(2,1)S(1)}, u32[]{:S(2)}, u32[]{:S(2)}) collective-permute-start(bf16[1,64,1,256]{3,1,2,0:T(8,128)(2,1)S(1)} %get-tuple-element.30), channel_id=1, source_target_pairs={{2,0},{4,2},{6,4},{3,1},{5,3},{7,5},{10,8},{12,10},{14,12},{11,9},... | collective-permute-start | bytes 98312 | tf_op jit(solution)/shard_map/ppermute | solution.py:15
  20.6 8.1 %collective-permute-start.3 = (bf16[1,64,34,1]{1,2,3,0:T(8,128)(2,1)S(1)}, bf16[1,64,34,1]{1,2,3,0:T(8,128)(2,1)S(1)}, u32[]{:S(2)}, u32[]{:S(2)}) collective-permute-start(bf16[1,64,34,1]{1,2,3,0:T(8,128)(2,1)S(1)} %copy.32), channel_id=1, source_target_pairs={{1,0},{3,2},{5,4},{7,6},{9,8},{11,10},{13,12},{15,14},{17,16},{19,... | collective-permute-start | bytes 13064 | tf_op jit(solution)/shard_map/ppermute | solution.py:15
  22.2 11.0 %collective-permute-start.2 = (bf16[1,64,34,1]{1,2,3,0:T(8,128)(2,1)S(1)}, bf16[1,64,34,1]{1,2,3,0:T(8,128)(2,1)S(1)}, u32[]{:S(2)}, u32[]{:S(2)}) collective-permute-start(bf16[1,64,34,1]{1,2,3,0:T(8,128)(2,1)S(1)} %copy.29), channel_id=1, source_target_pairs={{0,1},{2,3},{4,5},{6,7},{8,9},{10,11},{12,13},{14,15},{16,17},{18,... | collective-permute-start | bytes 13064 | tf_op jit(solution)/shard_map/ppermute | solution.py:14
  29.1 4.2 %copy-start.1 = (bf16[1,64,34,1]{3,1,2,0:T(8,128)(2,1)}, bf16[1,64,34,1]{3,1,2,0:T(8,128)(2,1)S(1)}, u32[]{:S(2)}) copy-start(bf16[1,64,34,1]{3,1,2,0:T(8,128)(2,1)S(1)} %copy.33) | copy-start | bytes 13060
  33.6 2.4 %copy-start.17 = (f32[32,256,64]{1,2,0:T(8,128)S(1)}, f32[32,256,64]{1,2,0:T(8,128)}, u32[]{:S(2)}) copy-start(f32[32,256,64]{1,2,0:T(8,128)} %fusion.86) | copy-start | bytes 6291460
  34.2 2.6 %copy-start.14 = (f32[32,256,64]{1,2,0:T(8,128)S(1)}, f32[32,256,64]{1,2,0:T(8,128)}, u32[]{:S(2)}) copy-start(f32[32,256,64]{1,2,0:T(8,128)} %fusion.58) | copy-start | bytes 6291460
  34.2 3.2 %copy-start.15 = (f32[32,256,64]{1,2,0:T(8,128)S(1)}, f32[32,256,64]{1,2,0:T(8,128)}, u32[]{:S(2)}) copy-start(f32[32,256,64]{1,2,0:T(8,128)} %fusion.61) | copy-start | bytes 6291460
  34.8 2.7 %copy-start.2 = (bf16[1,64,34,1]{3,1,2,0:T(8,128)(2,1)S(1)}, bf16[1,64,34,1]{3,1,2,0:T(8,128)(2,1)}, u32[]{:S(2)}) copy-start(bf16[1,64,34,1]{3,1,2,0:T(8,128)(2,1)} %copy-done.1) | copy-start | bytes 13060
  34.8 3.5 %copy-start.11 = (f32[32,256,64]{1,2,0:T(8,128)S(1)}, f32[32,256,64]{1,2,0:T(8,128)}, u32[]{:S(2)}) copy-start(f32[32,256,64]{1,2,0:T(8,128)} %fusion.55) | copy-start | bytes 6291460
  42.1 40.9 %copy-start = (f32[32,256,64]{1,2,0:T(8,128)}, f32[32,256,64]{1,2,0:T(8,128)S(1)}, u32[]{:S(2)}) copy-start(f32[32,256,64]{1,2,0:T(8,128)S(1)} %get-tuple-element.34) | copy-start | bytes 6291460
  42.1 40.9 %copy-start.21 = (f32[64]{0:T(128)S(1)}, f32[64]{0:T(128)}, u32[]{:S(2)}) copy-start(f32[64]{0:T(128)} %param.6) | copy-start | bytes 772
  83.0 2.8 %copy-start.19 = (f32[64]{0:T(128)}, f32[64]{0:T(128)S(1)}, u32[]{:S(2)}) copy-start(f32[64]{0:T(128)S(1)} %get-tuple-element.31) | copy-start | bytes 772
  83.0 2.8 %copy-start.20 = (f32[64]{0:T(128)}, f32[64]{0:T(128)S(1)}, u32[]{:S(2)}) copy-start(f32[64]{0:T(128)S(1)} %get-tuple-element.32) | copy-start | bytes 772
  83.0 2.8 %copy-start.5 = (bf16[1,64,34,1]{3,1,2,0:T(8,128)(2,1)S(1)}, bf16[1,64,34,1]{3,1,2,0:T(8,128)(2,1)}, u32[]{:S(2)}) copy-start(bf16[1,64,34,1]{3,1,2,0:T(8,128)(2,1)} %copy-done.4) | copy-start | bytes 13060
  95.0 6.6 %collective-permute-start.5 = (bf16[1,64,1,256]{3,1,2,0:T(8,128)(2,1)S(1)}, bf16[1,64,1,256]{3,1,2,0:T(8,128)(2,1)S(1)}, u32[]{:S(2)}, u32[]{:S(2)}) collective-permute-start(bf16[1,64,1,256]{3,1,2,0:T(8,128)(2,1)S(1)} %get-tuple-element.27), channel_id=1, source_target_pairs={{2,0},{4,2},{6,4},{3,1},{5,3},{7,5},{10,8},{12,10},{14,12},{11,9},... | collective-permute-start | bytes 98312 | tf_op jit(solution)/shard_map/ppermute | solution.py:15
  96.3 6.1 %collective-permute-start.4 = (bf16[1,64,1,256]{3,1,2,0:T(8,128)(2,1)S(1)}, bf16[1,64,1,256]{3,1,2,0:T(8,128)(2,1)S(1)}, u32[]{:S(2)}, u32[]{:S(2)}) collective-permute-start(bf16[1,64,1,256]{3,1,2,0:T(8,128)(2,1)S(1)} %get-tuple-element.28), channel_id=1, source_target_pairs={{0,2},{2,4},{4,6},{1,3},{3,5},{5,7},{8,10},{10,12},{12,14},{9,11},... | collective-permute-start | bytes 98312 | tf_op jit(solution)/shard_map/ppermute | solution.py:14
  103.2 8.5 %collective-permute-start.6 = (bf16[1,64,34,1]{1,2,3,0:T(8,128)(2,1)S(1)}, bf16[1,64,34,1]{1,2,3,0:T(8,128)(2,1)S(1)}, u32[]{:S(2)}, u32[]{:S(2)}) collective-permute-start(bf16[1,64,34,1]{1,2,3,0:T(8,128)(2,1)S(1)} %copy.37), channel_id=1, source_target_pairs={{1,0},{3,2},{5,4},{7,6},{9,8},{11,10},{13,12},{15,14},{17,16},{19,... | collective-permute-start | bytes 13064 | tf_op jit(solution)/shard_map/ppermute | solution.py:15
  104.8 7.3 %collective-permute-start.7 = (bf16[1,64,34,1]{1,2,3,0:T(8,128)(2,1)S(1)}, bf16[1,64,34,1]{1,2,3,0:T(8,128)(2,1)S(1)}, u32[]{:S(2)}, u32[]{:S(2)}) collective-permute-start(bf16[1,64,34,1]{1,2,3,0:T(8,128)(2,1)S(1)} %copy.41), channel_id=1, source_target_pairs={{0,1},{2,3},{4,5},{6,7},{8,9},{10,11},{12,13},{14,15},{16,17},{18,... | collective-permute-start | bytes 13064 | tf_op jit(solution)/shard_map/ppermute | solution.py:14
  116.0 2.5 %copy-start.10 = (f32[32,256,64]{1,2,0:T(8,128)S(1)}, f32[32,256,64]{1,2,0:T(8,128)}, u32[]{:S(2)}) copy-start(f32[32,256,64]{1,2,0:T(8,128)} %fusion.52) | copy-start | bytes 6291460
  (7 other events, 10.9 us)
Sparse Core Ops, SparseCore 0:
  101.8 23.6 reduce-scatter.1
where the time goes:
time: 163 us; the launch traced here: 162 us
  blocking collectives  70.7 us (43%)
  matrix products  31.1 us (19%)
  starting transfers between devices  21 us (13%)
  between operations  14.6 us (9%)
  local copies, waits for them, and re-layouts  13.5 us (8%)
  waiting for transfers between devices  6.31 us (4%)
  other arithmetic  5.31 us (3%)
    psum x1, blocking collectives, per_device(): lax.psum((local_pre, local_sq, local_cot, local_cross), ('dp', 'row', 'co...  40.6 us
    psum x1, blocking collectives, per_device(): spatial = lax.psum(local_kernel, ('row', 'col'))  30 us
    ppermute x4, starting transfers between devices, with_halo(): before = lax.ppermute(last, axis, up)  15.8 us
    dot_general x9, matrix products, per_device(): jnp.einsum('oc,bchw->bohw', kernel[tap_row, tap_col], window, preferred_e...  15.4 us
    unnamed x48, local copies, waits for them, and re-layouts  10.1 us
    dot_general x9, matrix products, per_device(): jnp.einsum('oc,bohw->bchw', kernel[tap_row, tap_col], shifted, preferred_...  9.7 us
    dot_general x9, matrix products, per_device(): jnp.einsum('bohw,bchw->oc', pre_grad, window, preferred_element_type=jnp....  5.99 us
    ppermute x4, starting transfers between devices, with_halo(): after = lax.ppermute(initial, axis, down)  5.16 us
  transfers between devices with their start and end apart: 9, of which 3 were waited for; matrix products, arithmetic and copies ran while one was open for 15% of the time, Pallas kernels for 0%

commit v1 on v0

v1 whole, which is shorter than its diff:
```python
import functools

import jax
import jax.numpy as jnp
from jax import lax
from jax.experimental import pallas as pl
from jax.experimental.pallas import tpu as pltpu
from jax.sharding import PartitionSpec as P

MESH = pl.DeviceIdType.MESH
F32 = jnp.float32
BF16 = jnp.bfloat16


def remote(src, dst, send, recv, device):
    return pltpu.make_async_remote_copy(
        src_ref=src, dst_ref=dst, send_sem=send, recv_sem=recv,
        device_id=device, device_id_type=MESH,
    )


def body(
    sizes, total,
    x_ref, cot_ref, wf_ref, wfe_ref, wb_ref, wbe_ref, gain_ref,
    out_ref, wg_ref, small_ref,
    xp, pre, x3, pgz, edge, rows_in, cols_out, cols_in, mine, grp, dps,
    acc, wdp, wpart, wgrp, wfin,
    row_s, row_r, col_s, col_r, ga_s, ga_r, gb_s, gb_r,
    wd_s, wd_r, wr_s, wr_r, wa_s, wa_r,
):
    n_dp, n_row, n_col = sizes
    n_grp = n_row * n_col
    height, channels, width = x_ref.shape
    half = width - 128
    dp, row, col = lax.axis_index("dp"), lax.axis_index("row"), lax.axis_index("col")
    me = row * n_col + col

    def member(k):
        k = lax.rem(me + k, n_grp)
        return k, (dp, k // n_col, lax.rem(k, n_col))

    def replica(k):
        k = lax.rem(dp + k, n_dp)
        return k, (k, row, col)

    barrier = pltpu.get_barrier_semaphore()
    for k in range(1, n_grp):
        pl.semaphore_signal(barrier, inc=1, device_id=member(k)[1], device_id_type=MESH)
    for k in range(1, n_dp):
        pl.semaphore_signal(barrier, inc=1, device_id=replica(k)[1], device_id_type=MESH)

    def sides(axis_pos, count, make):
        return ((axis_pos > 0, make(axis_pos - 1)), (axis_pos < count - 1, make(axis_pos + 1)))

    row_sides = sides(row, n_row, lambda r: (dp, r, col))
    col_sides = sides(col, n_col, lambda c: (dp, row, c))

    def exchange(which, near, sources, landing, send, recv):
        copies = []
        for s in range(2):
            exists, device = near[s]
            out = remote(sources[s], landing.at[which, 1 - s], send.at[which, s], recv.at[which, 1 - s], device)
            pl.when(exists)(out.start)
            copies.append(out)
        return copies

    def finish(which, near, sources, landing, send, recv):
        for s in range(2):
            exists, device = near[s]
            inc = remote(sources[s], landing.at[which, s], send.at[which, s], recv.at[which, s], device)

            @pl.when(exists)
            def _():
                inc.wait_send()
                inc.wait_recv()

    lanes = lax.broadcasted_iota(jnp.int32, (channels, 128), 1)

    def conv_row(src, w_ref, start):
        rhs = src[pl.ds(start, 3)].reshape(3 * channels, width)
        p = jnp.dot(w_ref[...], rhs, preferred_element_type=F32)
        wide = lax.broadcasted_iota(jnp.int32, (channels, width), 1)
        a = pltpu.roll(p[:channels], 1, 1)
        b = pltpu.roll(p[2 * channels :], width - 1, 1)
        a = jnp.where(wide == 0, 0.0, a)
        b = jnp.where(wide == width - 1, 0.0, b)
        return p[channels : 2 * channels] + a + b

    def columns(src, offset):
        def step(r, c):
            line = src[r + offset].astype(F32)
            last = pltpu.roll(line[:, half:], r + 1, 1)
            first = pltpu.roll(line[:, :128], 64 + r, 1)
            return jnp.where(lanes == r, last, jnp.where(lanes == 64 + r, first, c))

        return lax.fori_loop(0, height + 2, step, jnp.zeros((channels, 128), F32), unroll=2)

    def received(which):
        left = jnp.where(jnp.logical_and(lanes < 64, col > 0), cols_in[which, 0].astype(F32), 0.0)
        right = jnp.where(
            jnp.logical_and(lanes >= 64, col < n_col - 1), cols_in[which, 1].astype(F32), 0.0
        )
        return left + right

    def edge_terms(w_ref, c):
        g = jnp.dot(w_ref[...], c.astype(BF16), preferred_element_type=F32)
        left = jnp.zeros((channels, 128), F32)
        right = jnp.zeros((channels, 128), F32)
        for i in range(3):
            base = 3 * channels * i
            one, two = g[base : base + channels], g[base + 2 * channels : base + 3 * channels]
            if i:
                one, two = pltpu.roll(one, 128 - i, 1), pltpu.roll(two, 128 - i, 1)
            left, right = left + one, right + two
        return jnp.where(lanes < 64, left, right)

    def at_edges(values, r):
        left = jnp.where(lanes == 0, pltpu.roll(values, lax.rem(128 - r, 128), 1), 0.0)
        right = jnp.where(lanes == 127, pltpu.roll(values, lax.rem(191 - r, 128), 1), 0.0)
        return left, right

    def fill(h, _):
        xp[h + 1] = x_ref[h]
        return 0

    lax.fori_loop(0, height, fill, 0, unroll=4)
    zero_row = jnp.zeros((channels, width), BF16)
    for p in (0, 1, height + 2, height + 3):
        pgz[p] = zero_row

    pl.semaphore_wait(barrier, n_grp - 1 + n_dp - 1)
    x_rows = (x_ref.at[0], x_ref.at[height - 1])
    exchange(0, row_sides, x_rows, rows_in, row_s, row_r)

    def conv(h, _):
        pre[h] = conv_row(xp, wf_ref, h)
        return 0

    lax.fori_loop(1, height - 1, conv, 0, unroll=2)
    finish(0, row_sides, x_rows, rows_in, row_s, row_r)

    def place(dst, which, first, last):
        for s, p in ((0, first), (1, last)):

            @pl.when(row_sides[s][0])
            def _():
                dst[p] = rows_in[which, s]

            @pl.when(jnp.logical_not(row_sides[s][0]))
            def _():
                dst[p] = zero_row

    place(xp, 0, 0, height + 1)
    cols_out[0] = columns(xp, 0).astype(BF16)
    own_cols = (cols_out.at[0], cols_out.at[0])
    exchange(0, col_sides, own_cols, cols_in, col_s, col_r)
    conv(0, 0)
    conv(height - 1, 0)
    finish(0, col_sides, own_cols, cols_in, col_s, col_r)
    c = received(0)
    edge[0] = edge_terms(wfe_ref, c)
    edge[1] = c

    def stats(h, sums):
        left, right = at_edges(edge[0], h)
        p0 = pre[h, :, :128] + left
        pre[h, :, :128] = p0
        p1 = pre[h, :, half:] + right
        pre[h, :, half:] = p1
        g0, g1 = cot_ref[h, :, :128].astype(F32), cot_ref[h, :, half:].astype(F32)
        s0, s1, s2, s3 = sums
        return (s0 + (p0 + p1), s1 + (p0 * p0 + p1 * p1), s2 + (g0 + g1), s3 + (g0 * p0 + g1 * p1))

    empty = jnp.zeros((channels, 128), F32)
    sums = lax.fori_loop(0, height, stats, (empty, empty, empty, empty))
    mine[...] = jnp.zeros((8, 128), F32)
    for q in range(4):
        mine[q : q + 1, :channels] = jnp.sum(sums[q].T, axis=0, keepdims=True)

    def share(n, others, index, source, landing, send, recv):
        copies = []
        for k in range(1, n):
            peer, device = others(k)
            out = remote(source, landing.at[index], send.at[peer], recv.at[index], device)
            out.start()
        return copies

    def gather(n, others, index, source, landing, send, recv):
        for k in range(1, n):
            peer, device = others(k)
            inc = remote(source, landing.at[peer], send.at[peer], recv.at[peer], device)
            inc.wait_send()
            inc.wait_recv()

    share(n_grp, member, me, mine, grp, ga_s, ga_r)
    grp[me] = mine[...]

    def taps(r, _):
        line = xp[r].astype(F32)
        left, right = at_edges(edge[1], r)
        a = pltpu.roll(line, 1, 1)
        b = pltpu.roll(line, width - 1, 1)
        a0 = jnp.where(lanes == 0, left, a[:, :128])
        b1 = jnp.where(lanes == 127, right, b[:, half:])
        x3[r, :channels, :128] = a0.astype(BF16)
        x3[r, :channels, half:] = a[:, half:].astype(BF16)
        x3[r, channels : 2 * channels] = xp[r]
        x3[r, 2 * channels :, :128] = b[:, :128].astype(BF16)
        x3[r, 2 * channels :, half:] = b1.astype(BF16)
        return 0

    lax.fori_loop(0, height + 2, taps, 0, unroll=2)

    gather(n_grp, member, me, mine, grp, ga_s, ga_r)
    mine[...] = jnp.sum(grp[...], axis=0)
    share(n_dp, replica, dp, mine, dps, gb_s, gb_r)
    dps[dp] = mine[...]
    gather(n_dp, replica, dp, mine, dps, gb_s, gb_r)
    sums = jnp.sum(dps[...], axis=0)

    def derive(sum_pre, sum_sq, sum_cot, sum_cross):
        mean = sum_pre / total
        rstd = lax.rsqrt(sum_sq / total - mean * mean + 1e-05)
        sum_norm = (sum_cross - mean * sum_cot) * rstd
        return mean, rstd, sum_norm / total, sum_cot / total

    _, _, norm_row, cot_row = derive(*(sums[q : q + 1] for q in range(4)))
    small_ref[...] = jnp.concatenate([norm_row, cot_row, sums[2:]], axis=0)
    tall = [jnp.broadcast_to(sums[q : q + 1], (128, 128)).T[:channels] for q in range(4)]
    mean, rstd, norm, cmean = derive(*tall)
    scale = gain_ref[...] * rstd
    for k, v in enumerate((mean, rstd, norm, cmean, scale)):
        edge[2 + k] = v

    def grad_row(h, _):
        for a in (0, half):
            g = cot_ref[h, :, a : a + 128].astype(F32)
            normed = (pre[h, :, a : a + 128] - edge[2]) * edge[3]
            pgz[h + 2, :, a : a + 128] = (edge[6] * (g - edge[5] - normed * edge[4])).astype(BF16)
        return 0

    grad_row(0, 0)
    grad_row(height - 1, 0)
    g_rows = (pgz.at[2], pgz.at[height + 1])
    exchange(1, row_sides, g_rows, rows_in, row_s, row_r)
    lax.fori_loop(1, height - 1, grad_row, 0, unroll=2)

    acc[...] = jnp.zeros_like(acc)

    def weight(r, _):
        lhs = pgz[pl.ds(r, 3)].reshape(3 * channels, width)
        acc[...] += lax.dot_general(
            lhs, x3[r], (((1,), (1,)), ((), ())), preferred_element_type=F32
        ).reshape(acc.shape)
        return 0

    lax.fori_loop(0, height + 2, weight, 0, unroll=2)
    acc[...] = acc[...] * (total ** -0.5)
    part = channels // n_dp

    def slab(k):
        return acc.at[:, pl.ds(pl.multiple_of(k * part, 8), part), :]

    for k in range(1, n_dp):
        peer, device = replica(k)
        remote(slab(peer), wdp.at[dp], wd_s.at[peer], wd_r.at[dp], device).start()
    wdp[dp] = acc[:, pl.ds(pl.multiple_of(dp * part, 8), part), :]

    finish(1, row_sides, g_rows, rows_in, row_s, row_r)
    place(pgz, 1, 1, height + 2)
    cols_out[1] = columns(pgz, 1).astype(BF16)
    own_grads = (cols_out.at[1], cols_out.at[1])
    exchange(1, col_sides, own_grads, cols_in, col_s, col_r)

    for k in range(1, n_dp):
        peer, device = replica(k)
        inc = remote(slab(peer), wdp.at[peer], wd_s.at[peer], wd_r.at[peer], device)
        inc.wait_send()
        inc.wait_recv()
    tiles = wpart.shape[0]
    wpart[...] = jnp.sum(wdp[...], axis=0).reshape(wpart.shape)

    def owner(t):
        k = t % n_grp
        return k, (dp, k // n_col, k % n_col)

    for t in range(tiles):
        k, device = owner(t)

        @pl.when(me != k)
        def _():
            remote(wpart.at[t], wgrp.at[t // n_grp, me], wr_s.at[t], wr_r.at[t // n_grp, me], device).start()

        @pl.when(me == k)
        def _():
            wgrp[t // n_grp, me] = wpart[t]

    def back(h, _):
        pre[h] = conv_row(pgz, wb_ref, h + 1)
        return 0

    lax.fori_loop(0, height, back, 0, unroll=2)

    for t in range(tiles):
        k, device = owner(t)
        level = t // n_grp

        @pl.when(me != k)
        def _():
            remote(wpart.at[t], wgrp.at[level, me], wr_s.at[t], wr_r.at[level, me], device).wait_send()

        @pl.when(me == k)
        def _():
            for s in range(1, n_grp):
                peer, other = member(s)
                remote(wpart.at[t], wgrp.at[level, peer], wr_s.at[t], wr_r.at[level, peer], other).wait_recv()
            wfin[t] = jnp.sum(wgrp[level], axis=0)
            for s in range(1, n_grp):
                peer, other = member(s)
                remote(wfin.at[t], wfin.at[t], wa_s.at[t, peer], wa_r.at[t], other).start()

    finish(1, col_sides, own_grads, cols_in, col_s, col_r)
    edge[0] = edge_terms(wbe_ref, received(1))

    def store(h, _):
        left, right = at_edges(edge[0], h)
        out_ref[h, :, :128] = (pre[h, :, :128] + left).astype(BF16)
        out_ref[h, :, half:] = (pre[h, :, half:] + right).astype(BF16)
        return 0

    lax.fori_loop(0, height, store, 0, unroll=2)

    for t in range(tiles):
        k, device = owner(t)

        @pl.when(me == k)
        def _():
            for s in range(1, n_grp):
                peer, other = member(s)
                remote(wfin.at[t], wfin.at[t], wa_s.at[t, peer], wa_r.at[t], other).wait_send()

        @pl.when(me != k)
        def _():
            remote(wfin.at[t], wfin.at[t], wa_s.at[t, 0], wa_r.at[t], device).wait_recv()

    wg_ref[...] = wfin[...]


def per_device(sizes, activations, kernel, gain, cotangent):
    images, channels, height, width = activations.shape
    n_dp, n_row, n_col = sizes
    n_grp = n_row * n_col
    total = float(images * height * width * n_dp * n_grp)
    x = activations[0].transpose(1, 0, 2)
    cot = cotangent[0].transpose(1, 0, 2)
    wf = kernel.transpose(1, 2, 0, 3).reshape(3 * channels, 3 * channels)
    wfe = kernel.reshape(9 * channels, channels)
    flipped = kernel[::-1, ::-1].transpose(0, 1, 3, 2)
    wb = flipped.transpose(1, 2, 0, 3).reshape(3 * channels, 3 * channels)
    wbe = flipped.reshape(9 * channels, channels)
    gains = jnp.broadcast_to(gain[:, None], (channels, 128))
    part = channels // n_dp
    tiles = 3 * part // 8 if part >= 8 else 3
    tile_rows = 3 * part // tiles
    levels = -(-tiles // n_grp)
    dma = pltpu.SemaphoreType.DMA
    vmem = pl.BlockSpec(memory_space=pltpu.VMEM)
    out, wg, small = pl.pallas_call(
        functools.partial(body, sizes, total),
        out_shape=(
            jax.ShapeDtypeStruct((height, channels, width), BF16),
            jax.ShapeDtypeStruct((tiles, tile_rows, 3 * channels), F32),
            jax.ShapeDtypeStruct((8, 128), F32),
        ),
        in_specs=[vmem] * 7,
        out_specs=(vmem, vmem, vmem),
        scratch_shapes=[
            pltpu.VMEM((height + 2, channels, width), BF16),
            pltpu.VMEM((height, channels, width), F32),
            pltpu.VMEM((height + 2, 3 * channels, width), BF16),
            pltpu.VMEM((height + 4, channels, width), BF16),
            pltpu.VMEM((7, channels, 128), F32),
            pltpu.VMEM((2, 2, channels, width), BF16),
            pltpu.VMEM((2, channels, 128), BF16),
            pltpu.VMEM((2, 2, channels, 128), BF16),
            pltpu.VMEM((8, 128), F32),
            pltpu.VMEM((n_grp, 8, 128), F32),
            pltpu.VMEM((n_dp, 8, 128), F32),
            pltpu.VMEM((3, channels, 3 * channels), F32),
            pltpu.VMEM((n_dp, 3, part, 3 * channels), F32),
            pltpu.VMEM((tiles, tile_rows, 3 * channels), F32),
            pltpu.VMEM((levels, n_grp, tile_rows, 3 * channels), F32),
            pltpu.VMEM((tiles, tile_rows, 3 * channels), F32),
            dma((2, 2)), dma((2, 2)), dma((2, 2)), dma((2, 2)),
            dma((n_grp,)), dma((n_grp,)), dma((n_dp,)), dma((n_dp,)),
            dma((n_dp,)), dma((n_dp,)),
            dma((tiles,)), dma((levels, n_grp)),
            dma((tiles, n_grp)), dma((tiles,)),
        ],
        compiler_params=pltpu.CompilerParams(
            collective_id=0, has_side_effects=True, vmem_limit_bytes=40 * 1024 * 1024
        ),
    )(x, cot, wf, wfe, wb, wbe, gains)
    input_grad = out.transpose(1, 0, 2)[None]
    weight_grad = wg.reshape(3, part, 3, channels)[::-1].transpose(0, 2, 1, 3)
    return input_grad, weight_grad, small[0, :channels], small[1, :channels]


def solution(mesh):
    sizes = tuple(mesh.shape[a] for a in ("dp", "row", "col"))
    return jax.shard_map(
        functools.partial(per_device, sizes),
        mesh=mesh,
        in_specs=(P("dp", None, "row", "col"), P(), P(), P("dp", None, "row", "col")),
        out_specs=(P("dp", None, "row", "col"), P(None, None, "dp", None), P(), P()),
        check_vma=False,
    )
```

time: 163 us -> 49 us (0.30)
  blocking collectives: 70.7 us -> 0 us
  Pallas kernels: 0 us -> 39.6 us
  matrix products: 31.1 us -> 0 us
  starting transfers between devices: 21 us -> 0 us
  between operations: 14.6 us -> 0.7 us
  waiting for transfers between devices: 6.31 us -> 0 us
  other arithmetic: 5.31 us -> 0 us
  local copies, waits for them, and re-layouts: 13.5 us -> 8.42 us
    psum x2 -> x0, blocking collectives: 70.7 us -> none  [the longest x1 40.6 us: per_device(): lax.psum((local_pre, local_sq, local_cot, local_cross), ('dp', 'row', 'co...]
    pallas_call x0 -> x1, Pallas kernels: none -> 39.6 us  [per_device(): pl.pallas_call(functools.partial(body, sizes, total), out_shape=(jax.Shap...]
    dot_general x27 -> x0, matrix products: 31.1 us -> none  [the longest x9 15.4 us: per_device(): jnp.einsum('oc,bchw->bohw', kernel[tap_row, tap_col], window, preferred_e...]
    ppermute x8 -> x0, starting transfers between devices: 20.9 us -> none  [the longest x4 15.8 us: with_halo(): before = lax.ppermute(last, axis, up)]
    unnamed x48 -> x8, local copies, waits for them, and re-layouts: 10.1 us -> 3.58 us
    reduce_scatter x1 -> x0, waiting for transfers between devices: 3.82 us -> none  [per_device(): lax.psum_scatter(spatial, 'dp', scatter_dimension=2, tiled=True)]
    transpose x0 -> x5, local copies, waits for them, and re-layouts: none -> 3.67 us  [the longest x1 2.41 us: per_device(): cot = cotangent[0].transpose(1, 0, 2)]
    convert_element_type x1 -> x0, other arithmetic: 2.75 us -> none  [per_device(): pre_grad = pre_grad.astype(jnp.bfloat16)]
  transfers between devices with their start and end apart: 9 -> 0, of which waited for: 3 -> 0; matrix products, arithmetic and copies ran while one was open for 15% -> 0% of each run, Pallas kernels for 0% -> 0%
where the time goes in v1:
time: 49 us; the launch traced here: 48.8 us
  Pallas kernels  39.6 us (81%)
  local copies, waits for them, and re-layouts  8.42 us (17%)
  between operations  0.7 us (1%)
    pallas_call x1, Pallas kernels, per_device(): pl.pallas_call(functools.partial(body, sizes, total), out_shape=(jax.Shap...  39.6 us
    unnamed x8, local copies, waits for them, and re-layouts  3.58 us
    transpose x1, local copies, waits for them, and re-layouts, per_device(): cot = cotangent[0].transpose(1, 0, 2)  2.41 us
    transpose x1, local copies, waits for them, and re-layouts, per_device(): wf = kernel.transpose(1, 2, 0, 3).reshape(3 * channels, 3 * channels)  1.04 us

profile of v1, /device:TPU:0, one launch (start us, length us, event | category | flops | bytes accessed | tf_op | source)
XLA Modules:
  0.0 48.8 jit_solution(13099778290342402713)
XLA Ops:
  0.6 0.0 copy-start.2
  0.6 0.6 %copy-done.2 = f32[64]{0:T(128)S(1)} copy-done((f32[64]{0:T(128)S(1)}, f32[64]{0:T(128)}, u32[]{:S(2)}) %copy-start.2) | copy-done | bytes 280
  1.3 0.1 broadcast_in_dim.4.gain_ref
  1.4 1.0 %copy.17 = bf16[3,64,3,64]{3,2,1,0:T(4,128)(2,1)S(1)} copy(bf16[3,64,3,64]{3,1,0,2:T(8,128)(2,1)} %bitcast.24) | data formatting | bytes 147456 | tf_op jit(solution)/shard_map/transpose | solution.py:356
  2.4 0.0 copy-start
  2.4 0.0 copy-start.1
  2.4 0.2 reshape.24.wf_ref
  2.6 0.7 %copy-done = bf16[3,3,64,64]{3,2,1,0:T(8,128)(2,1)S(1)} copy-done((bf16[3,3,64,64]{3,2,1,0:T(8,128)(2,1)S(1)}, bf16[3,3,64,64]{3,2,1,0:T(8,128)(2,1)}, u32[]{:S(2)}) %copy-start) | copy-done | bytes 73752
  3.3 0.1 reverse_bitcast_fusion
  3.4 0.1 copy.19
  3.5 0.2 copy.18
  3.7 0.2 reshape.26.wb_ref
  3.9 0.0 copy-done.1
  3.9 2.4 %copy_bitcast_fusion = (bf16[32,64,256]{2,1,0:T(8,128)(2,1)S(1)}, bf16[32,64,256]{2,1,0:T(8,128)(2,1)S(1)}) fusion(bf16[1,64,32,256]{3,2,1,0:T(8,128)(2,1)S(1)} %copy-done.1, bf16[1,64,32,256]{3,2,1,0:T(8,128)(2,1)} %param.4), kind=kLoop, calls=%fused_computation | loop fusion | bytes 4194304 | tf_op jit(solution)/shard_map/transpose | solution.py:355
  6.3 39.6 %shard_map.75 = (bf16[32,64,256]{2,1,0:T(8,128)(2,1)S(1)}, f32[6,8,192]{2,1,0:T(8,128)S(1)}, f32[8,128]{1,0:T(8,128)S(1)}) custom-call(bf16[32,64,256]{2,1,0:T(8,128)(2,1)S(1)} %get-tuple-element.23.x_ref, bf16[32,64,256]{2,1,0:T(8,128)(2,1)S(1)} %get-tuple-element.22.cot_ref, bf16[192,192]{1,0:T(8,128)(2,1)S(1)} %reshape.24.wf_ref, ...), custom_call_target="tpu_custom_call" | custom-call | tf_op jit(solution)/shard_map/pallas_call | solution.py:368
  45.9 1.6 %copy.20 = bf16[1,64,32,256]{3,2,1,0:T(8,128)(2,1)} copy(bf16[1,64,32,256]{3,1,2,0:T(8,128)(2,1)S(1)} %bitcast.26) | data formatting | bytes 2097152
  47.5 0.5 %slice_bitcast_fusion = (f32[64]{0:T(128)}, f32[64]{0:T(128)}) fusion(f32[8,128]{1,0:T(8,128)S(1)} %get-tuple-element.9), kind=kLoop, calls=%fused_computation.5 | loop fusion | bytes 1024 | tf_op jit(solution)/shard_map/squeeze | solution.py:406
  48.0 0.1 reshape.28
  48.1 0.6 %copy.21 = f32[3,3,16,64]{3,2,1,0:T(8,128)} copy(f32[3,3,16,64]{3,1,2,0:T(4,128)S(1)} %reverse_bitcast_fusion.2) | data formatting | bytes 73728
  (1 shorter events, 0.0 us)
Async XLA Ops:
  0.6 0.7 %copy-start.2 = (f32[64]{0:T(128)S(1)}, f32[64]{0:T(128)}, u32[]{:S(2)}) copy-start(f32[64]{0:T(128)} %param.6) | copy-start | bytes 772
  2.4 0.9 %copy-start = (bf16[3,3,64,64]{3,2,1,0:T(8,128)(2,1)S(1)}, bf16[3,3,64,64]{3,2,1,0:T(8,128)(2,1)}, u32[]{:S(2)}) copy-start(bf16[3,3,64,64]{3,2,1,0:T(8,128)(2,1)} %param.5) | copy-start | bytes 221188
  2.4 1.5 %copy-start.1 = (bf16[1,64,32,256]{3,2,1,0:T(8,128)(2,1)S(1)}, bf16[1,64,32,256]{3,2,1,0:T(8,128)(2,1)}, u32[]{:S(2)}) copy-start(bf16[1,64,32,256]{3,2,1,0:T(8,128)(2,1)} %param.7) | copy-start | bytes 3145732

commit v2 on v1

--- a/solution.py
+++ b/solution.py
@@ -21,8 +21,9 @@
 
 def body(
     sizes, total,
-    x_ref, cot_ref, wf_ref, wfe_ref, wb_ref, wbe_ref, gain_ref,
-    out_ref, wg_ref, small_ref,
+    x_ref, cot_ref, wfe_ref, gain_ref,
+    out_ref, wg_ref, norm_ref, shift_ref,
+    wf_ref, wb_ref, wbe_ref,
     xp, pre, x3, pgz, edge, rows_in, cols_out, cols_in, mine, grp, dps,
     acc, wdp, wpart, wgrp, wfin,
     row_s, row_r, col_s, col_r, ga_s, ga_r, gb_s, gb_r,
@@ -93,7 +94,7 @@
             first = pltpu.roll(line[:, :128], 64 + r, 1)
             return jnp.where(lanes == r, last, jnp.where(lanes == 64 + r, first, c))
 
-        return lax.fori_loop(0, height + 2, step, jnp.zeros((channels, 128), F32), unroll=2)
+        return lax.fori_loop(0, height + 2, step, jnp.zeros((channels, 128), F32), unroll=8)
 
     def received(which):
         left = jnp.where(jnp.logical_and(lanes < 64, col > 0), cols_in[which, 0].astype(F32), 0.0)
@@ -115,8 +116,9 @@
         return jnp.where(lanes < 64, left, right)
 
     def at_edges(values, r):
-        left = jnp.where(lanes == 0, pltpu.roll(values, lax.rem(128 - r, 128), 1), 0.0)
-        right = jnp.where(lanes == 127, pltpu.roll(values, lax.rem(191 - r, 128), 1), 0.0)
+        spots = lanes[: values.shape[0]]
+        left = jnp.where(spots == 0, pltpu.roll(values, lax.rem(128 - r, 128), 1), 0.0)
+        right = jnp.where(spots == 127, pltpu.roll(values, lax.rem(191 - r, 128), 1), 0.0)
         return left, right
 
     def fill(h, _):
@@ -125,6 +127,20 @@
 
     lax.fori_loop(0, height, fill, 0, unroll=4)
     zero_row = jnp.zeros((channels, width), BF16)
+
+    def tap(i, j):
+        base = channels * (3 * i + j)
+        return wfe_ref[base : base + channels].astype(F32)
+
+    for j in range(3):
+        rows = slice(j * channels, (j + 1) * channels)
+        wf_ref[rows] = jnp.concatenate([tap(i, j) for i in range(3)], axis=1).astype(BF16)
+        back_taps = [tap(2 - i, 2 - j).T for i in range(3)]
+        wb_ref[rows] = jnp.concatenate(back_taps, axis=1).astype(BF16)
+        for i in range(3):
+            base = channels * (3 * i + j)
+            wbe_ref[base : base + channels] = back_taps[i].astype(BF16)
+
     for p in (0, 1, height + 2, height + 3):
         pgz[p] = zero_row
 
@@ -136,7 +152,7 @@
         pre[h] = conv_row(xp, wf_ref, h)
         return 0
 
-    lax.fori_loop(1, height - 1, conv, 0, unroll=2)
+    lax.fori_loop(1, height - 1, conv, 0, unroll=6)
     finish(0, row_sides, x_rows, rows_in, row_s, row_r)
 
     def place(dst, which, first, last):
@@ -161,18 +177,24 @@
     edge[0] = edge_terms(wfe_ref, c)
     edge[1] = c
 
-    def stats(h, sums):
-        left, right = at_edges(edge[0], h)
-        p0 = pre[h, :, :128] + left
-        pre[h, :, :128] = p0
-        p1 = pre[h, :, half:] + right
-        pre[h, :, half:] = p1
-        g0, g1 = cot_ref[h, :, :128].astype(F32), cot_ref[h, :, half:].astype(F32)
+    def stats(part, h, sums):
+        left, right = at_edges(edge[0, part], h)
+        p0 = pre[h, part, :128] + left
+        pre[h, part, :128] = p0
+        p1 = pre[h, part, half:] + right
+        pre[h, part, half:] = p1
+        g0, g1 = cot_ref[h, part, :128].astype(F32), cot_ref[h, part, half:].astype(F32)
         s0, s1, s2, s3 = sums
         return (s0 + (p0 + p1), s1 + (p0 * p0 + p1 * p1), s2 + (g0 + g1), s3 + (g0 * p0 + g1 * p1))
 
-    empty = jnp.zeros((channels, 128), F32)
-    sums = lax.fori_loop(0, height, stats, (empty, empty, empty, empty))
+    halves = []
+    for k in range(2):
+        part = slice(k * channels // 2, (k + 1) * channels // 2)
+        empty = jnp.zeros((channels // 2, 128), F32)
+        halves.append(
+            lax.fori_loop(0, height, functools.partial(stats, part), (empty,) * 4, unroll=4)
+        )
+    sums = [jnp.concatenate(pair, axis=0) for pair in zip(*halves)]
     mine[...] = jnp.zeros((8, 128), F32)
     for q in range(4):
         mine[q : q + 1, :channels] = jnp.sum(sums[q].T, axis=0, keepdims=True)
@@ -209,7 +231,7 @@
         x3[r, 2 * channels :, half:] = b1.astype(BF16)
         return 0
 
-    lax.fori_loop(0, height + 2, taps, 0, unroll=2)
+    lax.fori_loop(0, height + 2, taps, 0, unroll=4)
 
     gather(n_grp, member, me, mine, grp, ga_s, ga_r)
     mine[...] = jnp.sum(grp[...], axis=0)
@@ -225,10 +247,11 @@
         return mean, rstd, sum_norm / total, sum_cot / total
 
     _, _, norm_row, cot_row = derive(*(sums[q : q + 1] for q in range(4)))
-    small_ref[...] = jnp.concatenate([norm_row, cot_row, sums[2:]], axis=0)
+    norm_ref[...] = norm_row[:, :channels]
+    shift_ref[...] = cot_row[:, :channels]
     tall = [jnp.broadcast_to(sums[q : q + 1], (128, 128)).T[:channels] for q in range(4)]
     mean, rstd, norm, cmean = derive(*tall)
-    scale = gain_ref[...] * rstd
+    scale = jnp.broadcast_to(gain_ref[...], (128, channels)).T * rstd
     for k, v in enumerate((mean, rstd, norm, cmean, scale)):
         edge[2 + k] = v
 
@@ -247,14 +270,23 @@
 
     acc[...] = jnp.zeros_like(acc)
 
-    def weight(r, _):
-        lhs = pgz[pl.ds(r, 3)].reshape(3 * channels, width)
+    def weight(rows, r):
+        lhs = [pgz[pl.ds(r + k, 3)].reshape(3 * channels, width) for k in range(rows)]
+        rhs = [x3[r + k] for k in range(rows)]
         acc[...] += lax.dot_general(
-            lhs, x3[r], (((1,), (1,)), ((), ())), preferred_element_type=F32
+            jnp.concatenate(lhs, axis=1), jnp.concatenate(rhs, axis=1),
+            (((1,), (1,)), ((), ())), preferred_element_type=F32,
         ).reshape(acc.shape)
-        return 0
-
-    lax.fori_loop(0, height + 2, weight, 0, unroll=2)
+
+    whole = (height + 2) // 8
+
+    def weights(k, _):
+        weight(8, k * 8)
+        return 0
+
+    lax.fori_loop(0, whole, weights, 0)
+    if (height + 2) % 8:
+        weight((height + 2) % 8, whole * 8)
     acc[...] = acc[...] * (total ** -0.5)
     part = channels // n_dp
 
@@ -299,7 +331,7 @@
         pre[h] = conv_row(pgz, wb_ref, h + 1)
         return 0
 
-    lax.fori_loop(0, height, back, 0, unroll=2)
+    lax.fori_loop(0, height, back, 0, unroll=8)
 
     for t in range(tiles):
         k, device = owner(t)
@@ -328,7 +360,7 @@
         out_ref[h, :, half:] = (pre[h, :, half:] + right).astype(BF16)
         return 0
 
-    lax.fori_loop(0, height, store, 0, unroll=2)
+    lax.fori_loop(0, height, store, 0, unroll=8)
 
     for t in range(tiles):
         k, device = owner(t)
@@ -343,7 +375,11 @@
         def _():
             remote(wfin.at[t], wfin.at[t], wa_s.at[t, 0], wa_r.at[t], device).wait_recv()
 
-    wg_ref[...] = wfin[...]
+    tile_rows = wfin.shape[1]
+    for t in range(tiles):
+        a, o = divmod(t * tile_rows, channels // n_dp)
+        for j in range(3):
+            wg_ref[2 - a, j, o : o + tile_rows] = wfin[t, :, j * channels : (j + 1) * channels]
 
 
 def per_device(sizes, activations, kernel, gain, cotangent):
@@ -353,28 +389,27 @@
     total = float(images * height * width * n_dp * n_grp)
     x = activations[0].transpose(1, 0, 2)
     cot = cotangent[0].transpose(1, 0, 2)
-    wf = kernel.transpose(1, 2, 0, 3).reshape(3 * channels, 3 * channels)
-    wfe = kernel.reshape(9 * channels, channels)
-    flipped = kernel[::-1, ::-1].transpose(0, 1, 3, 2)
-    wb = flipped.transpose(1, 2, 0, 3).reshape(3 * channels, 3 * channels)
-    wbe = flipped.reshape(9 * channels, channels)
-    gains = jnp.broadcast_to(gain[:, None], (channels, 128))
+    taps = kernel.reshape(9 * channels, channels)
     part = channels // n_dp
     tiles = 3 * part // 8 if part >= 8 else 3
     tile_rows = 3 * part // tiles
     levels = -(-tiles // n_grp)
     dma = pltpu.SemaphoreType.DMA
     vmem = pl.BlockSpec(memory_space=pltpu.VMEM)
-    out, wg, small = pl.pallas_call(
+    out, weight_grad, norm, shift = pl.pallas_call(
         functools.partial(body, sizes, total),
         out_shape=(
             jax.ShapeDtypeStruct((height, channels, width), BF16),
-            jax.ShapeDtypeStruct((tiles, tile_rows, 3 * channels), F32),
-            jax.ShapeDtypeStruct((8, 128), F32),
+            jax.ShapeDtypeStruct((3, 3, part, channels), F32),
+            jax.ShapeDtypeStruct((1, channels), F32),
+            jax.ShapeDtypeStruct((1, channels), F32),
         ),
-        in_specs=[vmem] * 7,
-        out_specs=(vmem, vmem, vmem),
+        in_specs=[vmem] * 4,
+        out_specs=(vmem,) * 4,
         scratch_shapes=[
+            pltpu.VMEM((3 * channels, 3 * channels), BF16),
+            pltpu.VMEM((3 * channels, 3 * channels), BF16),
+            pltpu.VMEM((9 * channels, channels), BF16),
             pltpu.VMEM((height + 2, channels, width), BF16),
             pltpu.VMEM((height, channels, width), F32),
             pltpu.VMEM((height + 2, 3 * channels, width), BF16),
@@ -400,10 +435,9 @@
         compiler_params=pltpu.CompilerParams(
             collective_id=0, has_side_effects=True, vmem_limit_bytes=40 * 1024 * 1024
         ),
-    )(x, cot, wf, wfe, wb, wbe, gains)
+    )(x, cot, taps, gain[None])
     input_grad = out.transpose(1, 0, 2)[None]
-    weight_grad = wg.reshape(3, part, 3, channels)[::-1].transpose(0, 2, 1, 3)
-    return input_grad, weight_grad, small[0, :channels], small[1, :channels]
+    return input_grad, weight_grad, norm[0], shift[0]
 
 
 def solution(mesh):

time: 49 us -> 39.5 us (0.81)
  Pallas kernels: 39.6 us -> 32.1 us
  local copies, waits for them, and re-layouts: 8.42 us -> 6.61 us
    pallas_call x1, Pallas kernels: 39.6 us -> 32.1 us  [per_device(): pl.pallas_call(functools.partial(body, sizes, total), out_shape=(jax.Shap...]
    transpose x4 -> x0, local copies, waits for them, and re-layouts: 1.26 us -> none  [the longest x1 1.04 us: per_device(): wf = kernel.transpose(1, 2, 0, 3).reshape(3 * channels, 3 * channels)]
    squeeze x1 -> x0, local copies, waits for them, and re-layouts: 0.52 us -> none  [per_device(): return (input_grad, weight_grad, small[0, :channels], small[1, :channels])]
where the time goes in v2:
time: 39.5 us; the launch traced here: 39.3 us
  Pallas kernels  32.1 us (81%)
  local copies, waits for them, and re-layouts  6.61 us (17%)
  between operations  0.67 us (2%)
    pallas_call x1, Pallas kernels, per_device(): pl.pallas_call(functools.partial(body, sizes, total), out_shape=(jax.Shap...  32.1 us
    unnamed x8, local copies, waits for them, and re-layouts  3.85 us
    transpose x1, local copies, waits for them, and re-layouts, per_device(): cot = cotangent[0].transpose(1, 0, 2)  2.76 us

profile of v2, /device:TPU:0, one launch (start us, length us, event | category | flops | bytes accessed | tf_op | source)
XLA Modules:
  0.0 39.3 jit_solution(18059962497811951619)
XLA Ops:
  0.6 0.0 copy-start
  0.6 2.8 %copy_bitcast_fusion = (bf16[32,64,256]{2,1,0:T(8,128)(2,1)S(1)}, bf16[32,64,256]{2,1,0:T(8,128)(2,1)S(1)}) fusion(bf16[1,64,32,256]{3,2,1,0:T(8,128)(2,1)} %param.7, bf16[1,64,32,256]{3,2,1,0:T(8,128)(2,1)} %param.4), kind=kLoop, calls=%fused_computation | loop fusion | bytes 4194304 | tf_op jit(solution)/shard_map/transpose | solution.py:391
  3.4 0.0 copy-start.1
  3.4 0.0 copy-done
  3.4 0.6 %copy-done.1 = f32[64]{0:T(128)S(1)} copy-done((f32[64]{0:T(128)S(1)}, f32[64]{0:T(128)}, u32[]{:S(2)}) %copy-start.1) | copy-done | bytes 280
  4.1 32.1 %shard_map.75 = (bf16[32,64,256]{2,1,0:T(8,128)(2,1)S(1)}, f32[3,3,16,64]{3,2,1,0:T(8,128)S(1)}, f32[1,64]{1,0:T(1,128)S(1)}, f32[1,64]{1,0:T(1,128)S(1)}) custom-call(bf16[32,64,256]{2,1,0:T(8,128)(2,1)S(1)} %get-tuple-element.17.x_ref, bf16[32,64,256]{2,1,0:T(8,128)(2,1)S(1)} %get-tuple-element.16.cot_ref, bf16[576,64]{1,0:T(8,128)(2,1)S(1)} %bitcast.16, ...), custom_call_target="tpu_custom_call" | custom-call | tf_op jit(solution)/shard_map/pallas_call | solution.py:399
  36.1 1.6 %copy.10 = bf16[1,64,32,256]{3,2,1,0:T(8,128)(2,1)} copy(bf16[1,64,32,256]{3,1,2,0:T(8,128)(2,1)S(1)} %bitcast.15) | data formatting | bytes 2097152
  37.7 0.6 %copy.16 = f32[3,3,16,64]{3,2,1,0:T(8,128)} copy(f32[3,3,16,64]{3,2,1,0:T(8,128)S(1)} %get-tuple-element.23) | data formatting | bytes 73728
  38.3 0.5 %copy.17 = f32[64]{0:T(128)} copy(f32[64]{0:T(128)S(1)} %bitcast.19) | data formatting | bytes 512
  38.8 0.5 %copy.18 = f32[64]{0:T(128)} copy(f32[64]{0:T(128)S(1)} %bitcast.18) | data formatting | bytes 512
Async XLA Ops:
  0.6 2.8 %copy-start = (bf16[3,3,64,64]{3,2,1,0:T(8,128)(2,1)S(1)}, bf16[3,3,64,64]{3,2,1,0:T(8,128)(2,1)}, u32[]{:S(2)}) copy-start(bf16[3,3,64,64]{3,2,1,0:T(8,128)(2,1)} %param.5) | copy-start | bytes 221188
  3.4 0.7 %copy-start.1 = (f32[64]{0:T(128)S(1)}, f32[64]{0:T(128)}, u32[]{:S(2)}) copy-start(f32[64]{0:T(128)} %param.6) | copy-start | bytes 772

commit v3 on v2

--- a/solution.py
+++ b/solution.py
@@ -21,8 +21,9 @@
 
 def body(
     sizes, total,
-    x_ref, cot_ref, wfe_ref, gain_ref,
-    out_ref, wg_ref, norm_ref, shift_ref,
+    x_ref, cot_ref, taps_ref, gains_ref,
+    out_ref, wg_ref, small_ref,
+    wfe_ref, gain_ref, own_s,
     wf_ref, wb_ref, wbe_ref,
     xp, pre, x3, pgz, edge, rows_in, cols_out, cols_in, mine, grp, dps,
     acc, wdp, wpart, wgrp, wfin,
@@ -44,6 +45,10 @@
         k = lax.rem(dp + k, n_dp)
         return k, (k, row, col)
 
+    fetch_taps = pltpu.make_async_copy(taps_ref, wfe_ref, own_s.at[0])
+    fetch_gain = pltpu.make_async_copy(gains_ref, gain_ref, own_s.at[1])
+    fetch_taps.start()
+    fetch_gain.start()
     barrier = pltpu.get_barrier_semaphore()
     for k in range(1, n_grp):
         pl.semaphore_signal(barrier, inc=1, device_id=member(k)[1], device_id_type=MESH)
@@ -132,6 +137,8 @@
         base = channels * (3 * i + j)
         return wfe_ref[base : base + channels].astype(F32)
 
+    fetch_taps.wait()
+    fetch_gain.wait()
     for j in range(3):
         rows = slice(j * channels, (j + 1) * channels)
         wf_ref[rows] = jnp.concatenate([tap(i, j) for i in range(3)], axis=1).astype(BF16)
@@ -152,7 +159,7 @@
         pre[h] = conv_row(xp, wf_ref, h)
         return 0
 
-    lax.fori_loop(1, height - 1, conv, 0, unroll=6)
+    lax.fori_loop(1, height - 1, conv, 0, unroll=10)
     finish(0, row_sides, x_rows, rows_in, row_s, row_r)
 
     def place(dst, which, first, last):
@@ -192,7 +199,7 @@
         part = slice(k * channels // 2, (k + 1) * channels // 2)
         empty = jnp.zeros((channels // 2, 128), F32)
         halves.append(
-            lax.fori_loop(0, height, functools.partial(stats, part), (empty,) * 4, unroll=4)
+            lax.fori_loop(0, height, functools.partial(stats, part), (empty,) * 4, unroll=8)
         )
     sums = [jnp.concatenate(pair, axis=0) for pair in zip(*halves)]
     mine[...] = jnp.zeros((8, 128), F32)
@@ -247,8 +254,7 @@
         return mean, rstd, sum_norm / total, sum_cot / total
 
     _, _, norm_row, cot_row = derive(*(sums[q : q + 1] for q in range(4)))
-    norm_ref[...] = norm_row[:, :channels]
-    shift_ref[...] = cot_row[:, :channels]
+    small_ref[...] = jnp.concatenate([norm_row, cot_row, sums[2:]], axis=0)
     tall = [jnp.broadcast_to(sums[q : q + 1], (128, 128)).T[:channels] for q in range(4)]
     mean, rstd, norm, cmean = derive(*tall)
     scale = jnp.broadcast_to(gain_ref[...], (128, channels)).T * rstd
@@ -266,7 +272,7 @@
     grad_row(height - 1, 0)
     g_rows = (pgz.at[2], pgz.at[height + 1])
     exchange(1, row_sides, g_rows, rows_in, row_s, row_r)
-    lax.fori_loop(1, height - 1, grad_row, 0, unroll=2)
+    lax.fori_loop(1, height - 1, grad_row, 0, unroll=6)
 
     acc[...] = jnp.zeros_like(acc)
 
@@ -331,7 +337,7 @@
         pre[h] = conv_row(pgz, wb_ref, h + 1)
         return 0
 
-    lax.fori_loop(0, height, back, 0, unroll=8)
+    lax.fori_loop(0, height, back, 0, unroll=16)
 
     for t in range(tiles):
         k, device = owner(t)
@@ -396,17 +402,19 @@
     levels = -(-tiles // n_grp)
     dma = pltpu.SemaphoreType.DMA
     vmem = pl.BlockSpec(memory_space=pltpu.VMEM)
-    out, weight_grad, norm, shift = pl.pallas_call(
+    out, weight_grad, small = pl.pallas_call(
         functools.partial(body, sizes, total),
         out_shape=(
             jax.ShapeDtypeStruct((height, channels, width), BF16),
             jax.ShapeDtypeStruct((3, 3, part, channels), F32),
-            jax.ShapeDtypeStruct((1, channels), F32),
-            jax.ShapeDtypeStruct((1, channels), F32),
+            jax.ShapeDtypeStruct((8, 128), F32),
         ),
-        in_specs=[vmem] * 4,
-        out_specs=(vmem,) * 4,
+        in_specs=[vmem] * 2 + [pl.BlockSpec(memory_space=pl.ANY)] * 2,
+        out_specs=(vmem,) * 3,
         scratch_shapes=[
+            pltpu.VMEM((9 * channels, channels), BF16),
+            pltpu.VMEM((1, channels), F32),
+            dma((2,)),
             pltpu.VMEM((3 * channels, 3 * channels), BF16),
             pltpu.VMEM((3 * channels, 3 * channels), BF16),
             pltpu.VMEM((9 * channels, channels), BF16),
@@ -437,7 +445,7 @@
         ),
     )(x, cot, taps, gain[None])
     input_grad = out.transpose(1, 0, 2)[None]
-    return input_grad, weight_grad, norm[0], shift[0]
+    return input_grad, weight_grad, small[0, :channels], small[1, :channels]
 
 
 def solution(mesh):

time: 39.5 us -> 38.7 us (0.980)
  local copies, waits for them, and re-layouts: 6.61 us -> 6.1 us
  Pallas kernels: 32.1 us -> 31.7 us
    unnamed x8 -> x6, local copies, waits for them, and re-layouts: 3.85 us -> 2.83 us
    squeeze x0 -> x1, local copies, waits for them, and re-layouts: none -> 0.52 us  [per_device(): return (input_grad, weight_grad, small[0, :channels], small[1, :channels])]
where the time goes in v3:
time: 38.7 us; the launch traced here: 38.5 us
  Pallas kernels  31.7 us (82%)
  local copies, waits for them, and re-layouts  6.1 us (16%)
  between operations  0.67 us (2%)
    pallas_call x1, Pallas kernels, per_device(): pl.pallas_call(functools.partial(body, sizes, total), out_shape=(jax.Shap...  31.7 us
    unnamed x6, local copies, waits for them, and re-layouts  2.83 us
    transpose x1, local copies, waits for them, and re-layouts, per_device(): cot = cotangent[0].transpose(1, 0, 2)  2.76 us

profile of v3, /device:TPU:0, one launch (start us, length us, event | category | flops | bytes accessed | tf_op | source)
XLA Modules:
  0.0 38.5 jit_solution(15841343698704116324)
XLA Ops:
  0.6 0.0 copy-start
  0.6 2.8 %copy_bitcast_fusion = (bf16[32,64,256]{2,1,0:T(8,128)(2,1)S(1)}, bf16[32,64,256]{2,1,0:T(8,128)(2,1)S(1)}) fusion(bf16[1,64,32,256]{3,2,1,0:T(8,128)(2,1)} %param.7, bf16[1,64,32,256]{3,2,1,0:T(8,128)(2,1)} %param.4), kind=kLoop, calls=%fused_computation | loop fusion | bytes 4194304 | tf_op jit(solution)/shard_map/transpose | solution.py:397
  3.4 0.0 copy-start.1
  3.4 0.0 copy-done
  3.4 0.6 %copy-done.1 = f32[64]{0:T(128)S(1)} copy-done((f32[64]{0:T(128)S(1)}, f32[64]{0:T(128)}, u32[]{:S(2)}) %copy-start.1) | copy-done | bytes 280
  4.1 31.7 %shard_map.75 = (bf16[32,64,256]{2,1,0:T(8,128)(2,1)S(1)}, f32[3,3,16,64]{3,2,1,0:T(8,128)S(1)}, f32[8,128]{1,0:T(8,128)S(1)}) custom-call(bf16[32,64,256]{2,1,0:T(8,128)(2,1)S(1)} %get-tuple-element.17.x_ref, bf16[32,64,256]{2,1,0:T(8,128)(2,1)S(1)} %get-tuple-element.16.cot_ref, bf16[576,64]{1,0:T(8,128)(2,1)S(1)} %bitcast.18, f32[1,64]{1,0:T(1,128)S(1)} %bitcast.19), custom_call_target="tpu_custom_call" | custom-call | tf_op jit(solution)/shard_map/pallas_call | solution.py:405
  35.8 1.6 %copy.10 = bf16[1,64,32,256]{3,2,1,0:T(8,128)(2,1)} copy(bf16[1,64,32,256]{3,1,2,0:T(8,128)(2,1)S(1)} %bitcast.17) | data formatting | bytes 2097152
  37.4 0.5 %slice_bitcast_fusion = (f32[64]{0:T(128)}, f32[64]{0:T(128)}) fusion(f32[8,128]{1,0:T(8,128)S(1)} %get-tuple-element.9), kind=kLoop, calls=%fused_computation.2 | loop fusion | bytes 1024 | tf_op jit(solution)/shard_map/squeeze | solution.py:448
  37.9 0.6 %copy.14 = f32[3,3,16,64]{3,2,1,0:T(8,128)} copy(f32[3,3,16,64]{3,2,1,0:T(8,128)S(1)} %get-tuple-element.23) | data formatting | bytes 73728
Async XLA Ops:
  0.6 2.8 %copy-start = (bf16[3,3,64,64]{3,2,1,0:T(8,128)(2,1)S(1)}, bf16[3,3,64,64]{3,2,1,0:T(8,128)(2,1)}, u32[]{:S(2)}) copy-start(bf16[3,3,64,64]{3,2,1,0:T(8,128)(2,1)} %param.5) | copy-start | bytes 221188
  3.4 0.7 %copy-start.1 = (f32[64]{0:T(128)S(1)}, f32[64]{0:T(128)}, u32[]{:S(2)}) copy-start(f32[64]{0:T(128)} %param.6) | copy-start | bytes 772
